TPU v7x, 32 devices: a whole 2x2x4 slice. The times are simulated.
32 devices in a mesh: row: 2 (over x), col: 4 (over z), depth: 4 (over y, core).
Axes of the slice: x: 2, y: 2, z: 4, core: 2. Of those that a mesh axis runs over, the one named last changes fastest.
Arguments:
- spd_matrix: float32 [16384, 16384], P('row', ('col', 'depth')), may hold values from -8 to 24
Outputs:
- panel_factor: float32 [16384, 512], P('row')
- schur_part: float32 [16384, 16384], P('row', ('col', 'depth'))
All inputs are finite; a program needn't handle non-finite values.
Results may differ from a plain program's by a relative error of at most 0.00015.
Values sent between devices are 32-bit elements; how exact they have to be, the bound alone decides.
A program may use at most 192 MiB of HBM per device.

v0:
```python
import jax
import jax.numpy as jnp
from jax import lax
from jax.sharding import PartitionSpec as P

PANEL = 512


def from_root(block, axis, owner):
    block = jnp.where(lax.axis_index(axis) == owner, block, jnp.zeros_like(block))
    return lax.psum(block, axis)


def shards(spd_matrix):
    rows = spd_matrix.shape[0]
    top_block = from_root(spd_matrix[:PANEL, :], "row", 0)
    stacked = jnp.concatenate([spd_matrix[:, :PANEL], top_block[:, :PANEL]], axis=0)
    arrived = from_root(stacked, ("col", "depth"), 0)
    raw = arrived[:rows]
    pivot = arrived[rows:]
    pivot_factor = jnp.linalg.cholesky(pivot)
    mine = lax.linalg.triangular_solve(
        pivot_factor, raw, left_side=False, lower=True, transpose_a=True
    )
    matching_top = lax.linalg.triangular_solve(
        pivot_factor, top_block, left_side=True, lower=True, transpose_a=False
    )
    update = jnp.dot(
        mine, matching_top, precision=lax.Precision.HIGHEST, preferred_element_type=jnp.float32
    )
    return (mine, spd_matrix - update)


def solution(mesh):
    placed = (P("row", ("col", "depth")),)
    return jax.shard_map(
        shards,
        mesh=mesh,
        in_specs=placed,
        out_specs=(P("row", None), P("row", ("col", "depth"))),
        check_vma=False,
    )
```

profile of v0, /device:TPU:0, one launch (start us, length us, event | category | flops | bytes accessed | tf_op | source)
XLA Modules:
  0.0 700.0 jit_solution(10382602076195339939)
XLA Ops:
  13.8 11.9 %slice.142 = f32[8192,512]{1,0:T(8,128)} slice(f32[8192,1024]{1,0:T(8,128)} %param.1), slice={[0:8192], [0:512]} | slice | bytes 33554432 | tf_op jit(solution)/shard_map/slice | solution.py:17
  25.7 17.5 %copy.7 = f32[8192,512]{0,1:T(8,128)} copy(f32[8192,512]{1,0:T(8,128)} %slice.142) | data formatting | bytes 33554432
  43.2 35.4 %all-reduce.4.cloned.1.call-done = f32[512,1024]{0,1:T(8,128)} async-done(((f32[512,1024]{0,1:T(8,128)}), f32[512,1024]{0,1:T(8,128)}) %all-reduce.4.cloned.1.call-update) | async-done | bytes 2097168 | tf_op jit(solution)/shard_map/psum | solution.py:11
  79.9 11.8 %maximum_select_fusion = f32[8704,512]{0,1:T(8,128)} fusion(f32[512,512]{0,1:T(8,128)S(1)} %slice.157, f32[8192,512]{0,1:T(8,128)} %copy.7, pred[]{:T(512)S(6)} %eq.6), kind=kLoop, calls=%fused_computation.2 | loop fusion | flops 8912896 | bytes 35651584 | tf_op jit(solution)/shard_map/jit(_where)/select_n | solution.py:10
  91.8 313.8 %all-reduce.6.cloned.1.call-done = f32[8704,512]{0,1:T(8,128)} async-done(((f32[8704,512]{0,1:T(8,128)}), f32[8704,512]{0,1:T(8,128)}) %all-reduce.6.cloned.1.call-update) | async-done | bytes 17825808 | tf_op jit(solution)/shard_map/psum | solution.py:11
  409.6 11.7 %cholesky.104 = f32[128,128]{1,0:T(8,128)S(1)} custom-call(f32[128,128]{1,0:T(8,128)S(1)} %cholesky.266), custom_call_target="Cholesky" | custom-call | tf_op jit(solution)/shard_map/jit(cholesky)/cholesky | solution.py:21
  421.4 9.8 %custom-call.32 = f32[1,128,128]{1,2,0:T(8,128)S(1)} custom-call(f32[1,128,128]{2,1,0:T(8,128)S(1)} %get-tuple-element.31), custom_call_target="InvertDiagBlocksLowerTriangular" | custom-call | tf_op jit(solution)/shard_map/jit(cholesky)/cholesky | solution.py:21
  433.8 11.7 %cholesky.217 = f32[128,128]{1,0:T(8,128)S(1)} custom-call(f32[128,128]{1,0:T(8,128)S(1)} %cholesky.270), custom_call_target="Cholesky" | custom-call | tf_op jit(solution)/shard_map/jit(cholesky)/cholesky | solution.py:21
  445.6 10.2 %custom-call.33 = f32[1,128,128]{1,2,0:T(8,128)S(1)} custom-call(f32[1,128,128]{2,1,0:T(8,128)S(1)} %get-tuple-element.28), custom_call_target="InvertDiagBlocksLowerTriangular" | custom-call | tf_op jit(solution)/shard_map/jit(cholesky)/cholesky | solution.py:21
  457.4 11.7 %cholesky.238 = f32[128,128]{1,0:T(8,128)S(1)} custom-call(f32[128,128]{1,0:T(8,128)S(1)} %cholesky.275), custom_call_target="Cholesky" | custom-call | tf_op jit(solution)/shard_map/jit(cholesky)/cholesky | solution.py:21
  469.8 9.8 %custom-call.34 = f32[1,128,128]{1,2,0:T(8,128)S(1)} custom-call(f32[1,128,128]{2,1,0:T(8,128)S(1)} %get-tuple-element.25), custom_call_target="InvertDiagBlocksLowerTriangular" | custom-call | tf_op jit(solution)/shard_map/jit(cholesky)/cholesky | solution.py:21
  481.1 11.7 %cholesky.255 = f32[128,128]{1,0:T(8,128)S(1)} custom-call(f32[128,128]{1,0:T(8,128)S(1)} %convolution_subtract_fusion.7), custom_call_target="Cholesky" | custom-call | tf_op jit(solution)/shard_map/jit(cholesky)/cholesky | solution.py:21
  497.9 13.6 %while.1 = (s32[]{:T(128)}, f32[512,512]{1,0:T(8,128)}, s32[4,2]{0,1:T(2,128)S(1)}, f32[4,128,128]{2,1,0:T(8,128)}, s32[]{:T(128)}) while((s32[]{:T(128)}, f32[512,512]{1,0:T(8,128)}, s32[4,2]{0,1:T(2,128)S(1)}, f32[4,128,128]{2,1,0:T(8,128)}, s32[]{:T(128)}) %tuple.32), condition=%wide.while_cond, body=%wide.while_body.sunk | while | flops 2 | bytes 132705 | solution.py:22
  511.5 40.1 %custom-call.35 = f32[4,128,128]{1,2,0:T(8,128)S(1)} custom-call(f32[4,128,128]{2,1,0:T(8,128)} %get-tuple-element.9), custom_call_target="InvertDiagBlocksLowerTriangular" | custom-call | tf_op jit(solution)/shard_map/triangular_solve | solution.py:22
  562.8 5.9 fusion.12
  568.7 5.6 convolution_subtract_fusion.2
  574.3 4.2 fusion.52
  578.4 6.9 convolution_subtract_fusion.1
  585.4 4.2 fusion.54
  589.5 11.5 %fusion.6 = f32[8192,128]{0,1:T(8,128)} fusion(f32[8192,128]{0,1:T(8,128)S(1)} %fusion.54, f32[8192,128]{0,1:T(8,128)S(1)} %fusion.52, f32[8192,128]{0,1:T(8,128)S(1)} %fusion.12, f32[8704,512]{0,1:T(8,128)} %all-reduce.6.cloned.1.call-done, f32[512,512]{1,0:T(8,128)} %get-tuple-element.88), kind=kOutput, calls=%fused_computation.13 | convolution fusion | flops 4839178240 | bytes 21168128 | tf_op jit(solution)/shard_map/triangular_solve | solution.py:22
  601.0 5.6 fusion.56
  608.6 6.2 pad_maximum_fusion
  614.8 60.7 %convolution_subtract_fusion = f32[8192,1024]{1,0:T(8,128)} fusion(f32[8192,1024]{1,0:T(8,128)} %param.1, f32[128,1024]{1,0:T(8,128)S(1)} %fusion.55, f32[128,1024]{1,0:T(8,128)S(1)} %fusion.53, f32[128,1024]{1,0:T(8,128)S(1)} %fusion.51, f32[128,1024]{1,0:T(8,128)S(1)} %fusion.34, f32[8192,128]{0,1:T(8,128)} %copy-done, f32[8192,128]{0,1:T(8,128)S(1)} %fusion.54, ...), kind=kOutput, calls=%fused_computation.4 | convolution fusion | flops 51562151936 | bytes 85983232 | tf_op jit(solution)/shard_map/dot_general | solution.py:28
  675.5 17.4 %copy.6 = f32[8192,512]{1,0:T(8,128)} copy(f32[8192,512]{0,1:T(8,128)} %pad_maximum_fusion) | data formatting | bytes 33554432
  (58 shorter events, 47.5 us)
Async XLA Ops:
  7.2 1.6 slice-start
  7.2 71.5 %all-reduce.4.cloned.1.call-start = ((), (), s32[]{:S(2)}) async-start(), calls=%async_computation | async-start | bytes 4194304 | tf_op jit(solution)/shard_map/psum | solution.py:11
  13.7 391.8 %all-reduce.6.cloned.1.call-start = ((), (), s32[]{:S(2)}) async-start(), calls=%async_computation.1 | async-start | bytes 35651584 | tf_op jit(solution)/shard_map/psum | solution.py:11
  408.6 1.0 copy-start.2
  409.6 142.0 %copy-start.1 = (f32[512,1024]{0,1:T(8,128)S(1)}, f32[512,1024]{0,1:T(8,128)}, u32[]{:S(2)}) copy-start(f32[512,1024]{0,1:T(8,128)} %all-reduce.4.cloned.1.call-done) | copy-start | bytes 6291460
  606.6 2.0 copy-start
Sparse Core Ops, SparseCore 0:
  13.8 64.7 all-reduce.3
  91.9 313.6 all-reduce.5
where the time goes:
time: 711 us; the launch traced here: 700 us
  waiting for transfers between devices  349 us (49%)
  other arithmetic  143 us (20%)
  matrix products  121 us (17%)
  local copies, waits for them, and re-layouts  69.9 us (10%)
  between operations  17.1 us (2%)
    psum x2, waiting for transfers between devices, from_root(): return lax.psum(block, axis)  349 us
    another operation x14, other arithmetic, shards(): pivot_factor = jnp.linalg.cholesky(pivot)  78.8 us
    dot_general x1, matrix products, shards(): jnp.dot(mine, matching_top, precision=lax.Precision.HIGHEST, preferred_el...  60.7 us
    another operation x4, other arithmetic, shards(): lax.linalg.triangular_solve(pivot_factor, raw, left_side=False, lower=Tru...  47.4 us
    another operation x7, matrix products, shards(): lax.linalg.triangular_solve(pivot_factor, raw, left_side=False, lower=Tru...  43.8 us
    unnamed x9, local copies, waits for them, and re-layouts  39.7 us
    select_n x2, other arithmetic, from_root(): jnp.where(lax.axis_index(axis) == owner, block, jnp.zeros_like(block))  14.9 us
  transfers between devices with their start and end apart: 2, of which 2 were waited for; matrix products, arithmetic and copies ran while one was open for 4% of the time, Pallas kernels for 0%

commit v1 on v0

v1 whole, which is shorter than its diff:
```python
import functools

import jax
import jax.numpy as jnp
from jax import lax
from jax.experimental import pallas as pl
from jax.experimental.pallas import tpu as pltpu
from jax.sharding import PartitionSpec as P

PANEL = 512
NB = 128
PIECES = 8
MESH = pl.DeviceIdType.MESH
HIGHEST = lax.Precision.HIGHEST
CR = (((1,), (1,)), ((), ()))
CC = (((1,), (0,)), ((), ()))


def dot(a, b, dims=CC, precision=None):
    return lax.dot_general(a, b, dims, precision=precision, preferred_element_type=jnp.float32)


def split(x):
    hi = x.astype(jnp.bfloat16)
    return hi, (x - hi.astype(jnp.float32)).astype(jnp.bfloat16)


def dot3(a, b, dims=CC):
    (ah, al), (bh, bl) = a, b
    return dot(ah, bh, dims) + (dot(ah, bl, dims) + dot(al, bh, dims))


def block_inverse_factor(block):
    rows = lax.broadcasted_iota(jnp.int32, (NB, NB), 0)
    lanes = lax.broadcasted_iota(jnp.int32, (NB, NB), 1)
    a = block
    x = jnp.where(rows == lanes, 1.0, 0.0).astype(jnp.float32)
    sub = lax.broadcasted_iota(jnp.int32, (8, NB), 0)
    done = []
    for j in range(NB):
        r = j % 8
        row, xrow = a[r : r + 1, :], x[r : r + 1, :]
        s = lax.rsqrt(jnp.broadcast_to(row[:, j : j + 1], (1, NB)))
        row, xrow = row * s, xrow * s
        col = jnp.broadcast_to(a[:, j : j + 1], a.shape) * s
        head = jnp.where(sub > r, col[:8], 0.0)
        xhead = jnp.where(sub == r, xrow, x[:8] - head * xrow)
        if a.shape[0] > 8:
            tail = col[8:]
            xtail = x[8:] - tail * xrow
            atail = a[8:] - tail * row
            if r == 7:
                done.append(xhead)
                a, x = atail, xtail
            else:
                a = jnp.concatenate([a[:8] - head * row, atail], axis=0)
                x = jnp.concatenate([xhead, xtail], axis=0)
        else:
            a = a[:8] - head * row
            x = xhead
    done.append(x)
    return jnp.concatenate(done, axis=0)


def factor_kernel(pivot_ref, w_ref, a_ref):
    n = pivot_ref.shape[0]
    a_ref[...] = pivot_ref[...]
    rows = lax.broadcasted_iota(jnp.int32, (n, n), 0)
    lanes = lax.broadcasted_iota(jnp.int32, (n, n), 1)
    w_ref[...] = jnp.where(rows == lanes, 1.0, 0.0).astype(jnp.float32)
    below = lax.broadcasted_iota(jnp.int32, (n, NB), 0)

    @pl.loop(0, n // NB)
    def _(k):
        here = pl.ds(pl.multiple_of(k * NB, NB), NB)
        wkk = block_inverse_factor(a_ref[here, here])
        w_ref[here, :] = dot(wkk, w_ref[here, :], CC, HIGHEST)
        col = jnp.where(below >= (k + 1) * NB, a_ref[:, here], 0.0)
        col = dot(col, wkk, CR, HIGHEST)
        a_ref[...] -= dot(col, col, CR, HIGHEST)
        w_ref[...] -= dot(col, w_ref[here, :], CC, HIGHEST)


def inverse_factor(pivot):
    n = pivot.shape[0]
    return pl.pallas_call(
        factor_kernel,
        name="inverse_factor",
        out_shape=jax.ShapeDtypeStruct((n, n), jnp.float32),
        in_specs=[pl.BlockSpec(memory_space=pltpu.VMEM)],
        out_specs=pl.BlockSpec(memory_space=pltpu.VMEM),
        scratch_shapes=[pltpu.VMEM((n, n), jnp.float32)],
        cost_estimate=pl.CostEstimate(flops=60 * 10**9, bytes_accessed=2 * 4 * n * n, transcendentals=0),
    )(pivot)


def update_kernel(w_ref, top_ref, raw_ref, a_ref, panel_ref, out_ref, wh, wl, bh, bl):
    @pl.when(pl.program_id(0) == 0)
    def _():
        w = split(w_ref[...])
        wh[...], wl[...] = w
        bh[...], bl[...] = split(dot3(w, split(top_ref[...])))

    raw = split(raw_ref[0].T)
    panel = dot3(raw, (wh[...], wl[...]), CR)
    panel_ref[...] = panel
    out_ref[...] = a_ref[...] - dot3(split(panel), (bh[...], bl[...]))


def update(w, top, raw, a):
    chunks, n, width = raw.shape
    rows, cols = a.shape
    return pl.pallas_call(
        update_kernel,
        name="panel_and_update",
        grid=(chunks,),
        out_shape=(
            jax.ShapeDtypeStruct((rows, n), jnp.float32),
            jax.ShapeDtypeStruct((rows, cols), jnp.float32),
        ),
        in_specs=[
            pl.BlockSpec((n, n), lambda i: (0, 0)),
            pl.BlockSpec((n, cols), lambda i: (0, 0)),
            pl.BlockSpec((1, n, width), lambda i: (i, 0, 0)),
            pl.BlockSpec((width, cols), lambda i: (i, 0)),
        ],
        out_specs=(
            pl.BlockSpec((width, n), lambda i: (i, 0)),
            pl.BlockSpec((width, cols), lambda i: (i, 0)),
        ),
        scratch_shapes=[
            pltpu.VMEM((n, n), jnp.bfloat16),
            pltpu.VMEM((n, n), jnp.bfloat16),
            pltpu.VMEM((n, cols), jnp.bfloat16),
            pltpu.VMEM((n, cols), jnp.bfloat16),
        ],
        compiler_params=pltpu.CompilerParams(vmem_limit_bytes=50 * 2**20),
    )(w, top, raw, a)


def spread_kernel(groups, cols, depths, a_ref, out_ref, held, load_sem, send_sem, recv_sem, store_sem):
    n = held.shape[1] * PIECES
    size = n // PIECES
    r, c, d = lax.axis_index("row"), lax.axis_index("col"), lax.axis_index("depth")
    even = lax.rem(d, 2) == 0
    trunk = (c == 0) & even
    root = (r == 0) & (c == 0) & (d == 0)
    children = (
        ((r, lax.min(c + 1, cols - 1), d), even & (c < cols - 1)),
        ((r, c, lax.min(d + 2, depths - 1)), trunk & (d < depths - 2)),
        ((lax.min(r + 1, groups - 1), c, d), trunk & (d == 0) & (r < groups - 1)),
        ((r, c, lax.min(d + 1, depths - 1)), even),
    )
    parents = (
        ((r, lax.max(c - 1, 0), d), even & (c > 0)),
        ((r, c, lax.max(d - 2, 0)), trunk & (d > 0)),
        ((lax.max(r - 1, 0), c, d), trunk & (d == 0) & (r > 0)),
        ((r, c, lax.max(d - 1, 0)), lax.rem(d, 2) == 1),
    )
    barrier = pltpu.get_barrier_semaphore()
    for device, there in children + parents:

        @pl.when(there)
        def _(device=device):
            pl.semaphore_signal(barrier, inc=1, device_id=device, device_id_type=MESH)

    peers = sum(jnp.where(there, 1, 0) for _, there in children + parents)
    pl.semaphore_wait(barrier, peers)

    def load(p):
        return pltpu.make_async_copy(
            a_ref.at[pl.ds(p * size, size), pl.ds(0, n)], held.at[p], load_sem.at[p]
        )

    def send(p, k):
        return pltpu.make_async_remote_copy(
            src_ref=held.at[p],
            dst_ref=held.at[p],
            send_sem=send_sem.at[p, k],
            recv_sem=recv_sem.at[p],
            device_id=children[k][0],
            device_id_type=MESH,
        )

    def store(p):
        return pltpu.make_async_copy(held.at[p], out_ref.at[pl.ds(p * size, size)], store_sem.at[p])

    @pl.when(root)
    def _():
        for p in range(PIECES):
            load(p).start()

    for p in range(PIECES):

        @pl.when(root)
        def _():
            load(p).wait()

        @pl.when(jnp.logical_not(root))
        def _():
            send(p, 0).wait_recv()

        for k in range(4):

            @pl.when(children[k][1])
            def _():
                send(p, k).start()

        store(p).start()
    for p in range(PIECES):
        for k in range(4):

            @pl.when(children[k][1])
            def _():
                send(p, k).wait_send()

        store(p).wait()


def spread_pivot(groups, cols, depths, spd_matrix):
    n = PANEL
    return pl.pallas_call(
        functools.partial(spread_kernel, groups, cols, depths),
        name="spread_pivot",
        out_shape=jax.ShapeDtypeStruct((n, n), jnp.float32),
        in_specs=[pl.BlockSpec(memory_space=pl.ANY)],
        out_specs=pl.BlockSpec(memory_space=pl.ANY),
        scratch_shapes=[
            pltpu.VMEM((PIECES, n // PIECES, n), jnp.float32),
            pltpu.SemaphoreType.DMA((PIECES,)),
            pltpu.SemaphoreType.DMA((PIECES, 4)),
            pltpu.SemaphoreType.DMA((PIECES,)),
            pltpu.SemaphoreType.DMA((PIECES,)),
        ],
        compiler_params=pltpu.CompilerParams(collective_id=0, has_side_effects=True),
        cost_estimate=pl.CostEstimate(flops=10**10, bytes_accessed=8 * n * n, transcendentals=0),
    )(spd_matrix)


def shards(groups, colsplit, depths, spd_matrix):
    blocks = colsplit * depths
    axes = ("row", "col", "depth")
    cols = spd_matrix.shape[1]
    width = cols // groups
    row = lax.axis_index("row")
    place = row * blocks + lax.axis_index(("col", "depth"))
    mine = spd_matrix[:PANEL, :]

    pivot = spread_pivot(groups, colsplit, depths, spd_matrix)

    arrived = []
    for h in range(groups):
        pairs = [(q // groups, q) for q in range(h, groups * blocks, groups)]
        arrived.append(lax.ppermute(mine[:, h * width : (h + 1) * width], axes, pairs))
    arrived, pivot = lax.optimization_barrier((arrived, pivot))
    piece = arrived[0]
    for h in range(1, groups):
        piece = jnp.where(lax.rem(place, groups) == h, arrived[h], piece)
    piece, mine = lax.optimization_barrier((piece, mine))
    raw = lax.all_gather(piece, ("col", "depth"), axis=0, tiled=False)

    if groups == 2:
        got = lax.ppermute(mine, "row", [(0, 1)])
        top = jnp.where(row == 0, mine, got)
    else:
        top = lax.psum(jnp.where(row == 0, mine, 0.0), "row")

    w = inverse_factor(pivot)
    return update(w, top, raw, spd_matrix)


def solution(mesh):
    groups = mesh.shape["row"]
    placed = (P("row", ("col", "depth")),)
    return jax.shard_map(
        functools.partial(shards, groups, mesh.shape["col"], mesh.shape["depth"]),
        mesh=mesh,
        in_specs=placed,
        out_specs=(P("row", None), P("row", ("col", "depth"))),
        check_vma=False,
    )
```

time: 711 us -> 279 us (0.39); the launches traced: 700 us -> 278 us
  waiting for transfers between devices: 349 us -> 77.9 us
  Pallas kernels: 0 us -> 156 us
  other arithmetic: 143 us -> 4.5 us
  matrix products: 121 us -> 0 us
  local copies, waits for them, and re-layouts: 69.9 us -> 4.82 us
  starting transfers between devices: 0.08 us -> 20.3 us
    psum x2 -> x0, waiting for transfers between devices: 349 us -> none  [from_root(): return lax.psum(block, axis)]
    pallas_call x0 -> x3, Pallas kernels: none -> 156 us  [the longest x1 55.3 us: inverse_factor(): pl.pallas_call(factor_kernel, name='inverse_factor', out_shape=jax.ShapeD...]
    another operation x18 -> x0, other arithmetic: 126 us -> none  [the longest x14 78.8 us: shards(): pivot_factor = jnp.linalg.cholesky(pivot)]
    all_gather x0 -> x1, waiting for transfers between devices: none -> 77.8 us  [shards(): raw = lax.all_gather(piece, ('col', 'depth'), axis=0, tiled=False)]
    dot_general x1 -> x0, matrix products: 60.7 us -> none  [shards(): jnp.dot(mine, matching_top, precision=lax.Precision.HIGHEST, preferred_el...]
    another operation x20 -> x0, matrix products: 60.3 us -> none  [the longest x7 43.8 us: shards(): lax.linalg.triangular_solve(pivot_factor, raw, left_side=False, lower=Tru...]
    unnamed x9 -> x4, local copies, waits for them, and re-layouts: 39.7 us -> 0.01 us
    ppermute x0 -> x3, starting transfers between devices: none -> 20.2 us  [the longest x2 12 us: shards(): lax.ppermute(mine[:, h * width:(h + 1) * width], axes, pairs)]
  transfers between devices with their start and end apart: 2 -> 4, of which waited for: 2 -> 1; matrix products, arithmetic and copies ran while one was open for 4% -> 1% of each run, Pallas kernels for 0% -> 38%
where the time goes in v1:
time: 279 us; the launch traced here: 278 us
  Pallas kernels  156 us (56%)
  waiting for transfers between devices  77.9 us (28%)
  starting transfers between devices  20.3 us (7%)
  between operations  14.1 us (5%)
  local copies, waits for them, and re-layouts  4.82 us (2%)
  other arithmetic  4.5 us (2%)
    all_gather x1, waiting for transfers between devices, shards(): raw = lax.all_gather(piece, ('col', 'depth'), axis=0, tiled=False)  77.8 us
    pallas_call x1, Pallas kernels, inverse_factor(): pl.pallas_call(factor_kernel, name='inverse_factor', out_shape=jax.ShapeD...  55.3 us
    pallas_call x1, Pallas kernels, update(): pl.pallas_call(update_kernel, name='panel_and_update', grid=(chunks,), ou...  50.8 us
    pallas_call x1, Pallas kernels, spread_pivot(): pl.pallas_call(functools.partial(spread_kernel, groups, cols, depths), na...  50.3 us
    ppermute x2, starting transfers between devices, shards(): lax.ppermute(mine[:, h * width:(h + 1) * width], axes, pairs)  12 us
    ppermute x1, starting transfers between devices, shards(): got = lax.ppermute(mine, 'row', [(0, 1)])  8.26 us
  transfers between devices with their start and end apart: 4, of which 1 were waited for; matrix products, arithmetic and copies ran while one was open for 1% of the time, Pallas kernels for 38%

profile of v1, /device:TPU:0, one launch (start us, length us, event | category | flops | bytes accessed | tf_op | source)
XLA Modules:
  0.0 278.0 jit_solution(8995431272607957037)
XLA Ops:
  7.2 0.0 all-gather.3.cloned.1.call-start
  7.2 3.1 %fusion = (f32[512,512]{1,0:T(8,128)}, f32[512,512]{1,0:T(8,128)}) fusion(f32[8192,1024]{1,0:T(8,128)} %a_ref.3), kind=kLoop, calls=%fused_computation.2 | loop fusion | bytes 4194304 | tf_op jit(solution)/shard_map/slice | solution.py:254
  10.3 2.5 collective-permute-start.1
  12.8 9.5 %collective-permute-start = (f32[512,512]{1,0:T(8,128)}, f32[512,512]{1,0:T(8,128)}, u32[]{:S(2)}, u32[]{:S(2)}) collective-permute-start(f32[512,512]{1,0:T(8,128)} %get-tuple-element.13), channel_id=1, source_target_pairs={{0,0},{1,2},{2,4},{3,6},{4,8},{5,10},{6,12},{7,14},{8,16},{9,18},{... | collective-permute-start | bytes 3145736 | tf_op jit(solution)/shard_map/ppermute | solution.py:254
  22.3 1.7 slice.13
  24.0 0.0 copy-start.1
  24.0 50.3 %spread_pivot.1.pivot_ref = f32[512,512]{1,0:T(8,128)} custom-call(f32[8192,1024]{1,0:T(8,128)} %a_ref.3), custom_call_target="tpu_custom_call" | custom-call | flops 10000000000 | bytes 2097152 | tf_op jit(solution)/shard_map/spread_pivot/pallas_call | solution.py:222
  74.4 0.0 collective-permute-done.1
  74.4 0.0 collective-permute-done
  74.4 2.4 broadcast_select_fusion.1
  76.8 0.0 all-gather.3.cloned.1.call-update
  76.8 0.0 copy-done.1
  76.8 8.3 %collective-permute-start.2 = (f32[512,1024]{1,0:T(8,128)S(1)}, f32[512,1024]{1,0:T(8,128)}, u32[]{:S(2)}, u32[]{:S(2)}) collective-permute-start(f32[512,1024]{1,0:T(8,128)S(1)} %slice.13), channel_id=1, source_target_pairs={{0,16},{1,17},{2,18},{3,19},{4,20},{5,21},{6,22},{7,23},{8,24},{9,... | collective-permute-start | bytes 6291464 | tf_op jit(solution)/shard_map/ppermute | solution.py:263
  85.1 55.3 %inverse_factor.1.w_ref = f32[512,512]{1,0:T(8,128)} custom-call(f32[512,512]{1,0:T(8,128)} %spread_pivot.1.pivot_ref), custom_call_target="tpu_custom_call" | custom-call | flops 60000002048 | bytes 2097152 | tf_op jit(solution)/shard_map/inverse_factor/pallas_call | solution.py:86
  140.4 0.0 copy-start
  140.4 0.0 collective-permute-done.2
  140.4 2.1 broadcast_select_fusion.top_ref
  142.5 77.8 %all-gather.3.cloned.1.call-done = f32[8192,512]{1,0:T(8,128)} async-done(((f32[512,512]{1,0:T(8,128)}), f32[8192,512]{1,0:T(8,128)}) %all-gather.3.cloned.1.call-update) | async-done | bytes 16777232 | tf_op jit(solution)/shard_map/all_gather | solution.py:260
  220.3 0.0 copy-done
  220.3 50.8 %panel_and_update.1 = (f32[8192,512]{1,0:T(8,128)}, f32[8192,1024]{1,0:T(8,128)}) custom-call(f32[512,512]{1,0:T(8,128)S(1)} %copy-done, f32[512,1024]{1,0:T(8,128)S(1)} %broadcast_select_fusion.top_ref, f32[16,512,512]{2,1,0:T(8,128)} %bitcast.1, f32[8192,1024]{1,0:T(8,128)} %a_ref.3), custom_call_target="tpu_custom_call" | custom-call | tf_op jit(solution)/shard_map/panel_and_update/pallas_call | solution.py:113
Async XLA Ops:
  7.2 213.1 %all-gather.3.cloned.1.call-start = ((), (), s32[]{:S(2)}) async-start(), calls=%async_computation | async-start | bytes 17825792 | tf_op jit(solution)/shard_map/all_gather | solution.py:260
  10.3 64.1 %collective-permute-start.1 = (f32[512,512]{1,0:T(8,128)}, f32[512,512]{1,0:T(8,128)S(1)}, u32[]{:S(2)}, u32[]{:S(2)}) collective-permute-start(f32[512,512]{1,0:T(8,128)} %get-tuple-element.12), channel_id=1, source_target_pairs={{0,1},{1,3},{2,5},{3,7},{4,9},{5,11},{6,13},{7,15},{8,17},{9,19},{... | collective-permute-start | bytes 3145736 | tf_op jit(solution)/shard_map/ppermute | solution.py:254
  12.8 61.6 %collective-permute-start = (f32[512,512]{1,0:T(8,128)}, f32[512,512]{1,0:T(8,128)}, u32[]{:S(2)}, u32[]{:S(2)}) collective-permute-start(f32[512,512]{1,0:T(8,128)} %get-tuple-element.13), channel_id=1, source_target_pairs={{0,0},{1,2},{2,4},{3,6},{4,8},{5,10},{6,12},{7,14},{8,16},{9,18},{... | collective-permute-start | bytes 3145736 | tf_op jit(solution)/shard_map/ppermute | solution.py:254
  24.0 52.9 %copy-start.1 = (f32[512,1024]{1,0:T(8,128)}, f32[512,1024]{1,0:T(8,128)S(1)}, u32[]{:S(2)}) copy-start(f32[512,1024]{1,0:T(8,128)S(1)} %slice.13) | copy-start | bytes 6291460
  76.8 63.5 %collective-permute-start.2 = (f32[512,1024]{1,0:T(8,128)S(1)}, f32[512,1024]{1,0:T(8,128)}, u32[]{:S(2)}, u32[]{:S(2)}) collective-permute-start(f32[512,1024]{1,0:T(8,128)S(1)} %slice.13), channel_id=1, source_target_pairs={{0,16},{1,17},{2,18},{3,19},{4,20},{5,21},{6,22},{7,23},{8,24},{9,... | collective-permute-start | bytes 6291464 | tf_op jit(solution)/shard_map/ppermute | solution.py:263
  140.4 79.9 %copy-start = (f32[512,512]{1,0:T(8,128)S(1)}, f32[512,512]{1,0:T(8,128)}, u32[]{:S(2)}) copy-start(f32[512,512]{1,0:T(8,128)} %inverse_factor.1.w_ref) | copy-start | bytes 3145732
Sparse Core Ops, SparseCore 0:
  77.0 143.3 all-gather.2

commit v2 on v1

--- a/solution.py
+++ b/solution.py
@@ -102,7 +102,14 @@
         bh[...], bl[...] = split(dot3(w, split(top_ref[...])))
 
     raw = split(raw_ref[0].T)
-    panel = dot3(raw, (wh[...], wl[...]), CR)
+    half = wh.shape[0] // 2
+    panel = jnp.concatenate(
+        [
+            dot3([p[:, :half] for p in raw], (wh[:half, :half], wl[:half, :half]), CR),
+            dot3(raw, (wh[half:, :], wl[half:, :]), CR),
+        ],
+        axis=1,
+    )
     panel_ref[...] = panel
     out_ref[...] = a_ref[...] - dot3(split(panel), (bh[...], bl[...]))
 

time: 279 us -> 292 us (1.047)
  Pallas kernels: 156 us -> 170 us
    pallas_call x1, Pallas kernels: 50.8 us -> 64.2 us  [update(): pl.pallas_call(update_kernel, name='panel_and_update', grid=(chunks,), ou...]
  transfers between devices with their start and end apart: 4 -> 4, of which waited for: 1 -> 1; matrix products, arithmetic and copies ran while one was open for 1% -> 1% of each run, Pallas kernels for 38% -> 36%
where the time goes in v2:
time: 292 us; the launch traced here: 291 us
  Pallas kernels  170 us (58%)
  waiting for transfers between devices  77.9 us (27%)
  starting transfers between devices  20.3 us (7%)
  between operations  14.1 us (5%)
  local copies, waits for them, and re-layouts  4.82 us (2%)
  other arithmetic  4.5 us (2%)
    all_gather x1, waiting for transfers between devices, shards(): raw = lax.all_gather(piece, ('col', 'depth'), axis=0, tiled=False)  77.8 us
    pallas_call x1, Pallas kernels, update(): pl.pallas_call(update_kernel, name='panel_and_update', grid=(chunks,), ou...  64.2 us
    pallas_call x1, Pallas kernels, inverse_factor(): pl.pallas_call(factor_kernel, name='inverse_factor', out_shape=jax.ShapeD...  55.3 us
    pallas_call x1, Pallas kernels, spread_pivot(): pl.pallas_call(functools.partial(spread_kernel, groups, cols, depths), na...  50.3 us
    ppermute x2, starting transfers between devices, shards(): lax.ppermute(mine[:, h * width:(h + 1) * width], axes, pairs)  12 us
    ppermute x1, starting transfers between devices, shards(): got = lax.ppermute(mine, 'row', [(0, 1)])  8.26 us
  transfers between devices with their start and end apart: 4, of which 1 were waited for; matrix products, arithmetic and copies ran while one was open for 1% of the time, Pallas kernels for 36%

profile of v2, /device:TPU:0, one launch (start us, length us, event | category | flops | bytes accessed | tf_op | source)
XLA Modules:
  0.0 291.3 jit_solution(4202573972473067728)
XLA Ops:
  7.2 0.0 all-gather.3.cloned.1.call-start
  7.2 3.1 %fusion = (f32[512,512]{1,0:T(8,128)}, f32[512,512]{1,0:T(8,128)}) fusion(f32[8192,1024]{1,0:T(8,128)} %a_ref.3), kind=kLoop, calls=%fused_computation.2 | loop fusion | bytes 4194304 | tf_op jit(solution)/shard_map/slice | solution.py:261
  10.3 2.5 collective-permute-start.1
  12.8 9.5 %collective-permute-start = (f32[512,512]{1,0:T(8,128)}, f32[512,512]{1,0:T(8,128)}, u32[]{:S(2)}, u32[]{:S(2)}) collective-permute-start(f32[512,512]{1,0:T(8,128)} %get-tuple-element.13), channel_id=1, source_target_pairs={{0,0},{1,2},{2,4},{3,6},{4,8},{5,10},{6,12},{7,14},{8,16},{9,18},{... | collective-permute-start | bytes 3145736 | tf_op jit(solution)/shard_map/ppermute | solution.py:261
  22.3 1.7 slice.13
  24.0 0.0 copy-start.1
  24.0 50.3 %spread_pivot.1.pivot_ref = f32[512,512]{1,0:T(8,128)} custom-call(f32[8192,1024]{1,0:T(8,128)} %a_ref.3), custom_call_target="tpu_custom_call" | custom-call | flops 10000000000 | bytes 2097152 | tf_op jit(solution)/shard_map/spread_pivot/pallas_call | solution.py:229
  74.4 0.0 collective-permute-done.1
  74.4 0.0 collective-permute-done
  74.4 2.4 broadcast_select_fusion.1
  76.8 0.0 all-gather.3.cloned.1.call-update
  76.8 0.0 copy-done.1
  76.8 8.3 %collective-permute-start.2 = (f32[512,1024]{1,0:T(8,128)S(1)}, f32[512,1024]{1,0:T(8,128)}, u32[]{:S(2)}, u32[]{:S(2)}) collective-permute-start(f32[512,1024]{1,0:T(8,128)S(1)} %slice.13), channel_id=1, source_target_pairs={{0,16},{1,17},{2,18},{3,19},{4,20},{5,21},{6,22},{7,23},{8,24},{9,... | collective-permute-start | bytes 6291464 | tf_op jit(solution)/shard_map/ppermute | solution.py:270
  85.1 55.3 %inverse_factor.1.w_ref = f32[512,512]{1,0:T(8,128)} custom-call(f32[512,512]{1,0:T(8,128)} %spread_pivot.1.pivot_ref), custom_call_target="tpu_custom_call" | custom-call | flops 60000002048 | bytes 2097152 | tf_op jit(solution)/shard_map/inverse_factor/pallas_call | solution.py:86
  140.4 0.0 copy-start
  140.4 0.0 collective-permute-done.2
  140.4 2.1 broadcast_select_fusion.top_ref
  142.5 77.8 %all-gather.3.cloned.1.call-done = f32[8192,512]{1,0:T(8,128)} async-done(((f32[512,512]{1,0:T(8,128)}), f32[8192,512]{1,0:T(8,128)}) %all-gather.3.cloned.1.call-update) | async-done | bytes 16777232 | tf_op jit(solution)/shard_map/all_gather | solution.py:267
  220.3 0.0 copy-done
  220.3 64.2 %panel_and_update.1 = (f32[8192,512]{1,0:T(8,128)}, f32[8192,1024]{1,0:T(8,128)}) custom-call(f32[512,512]{1,0:T(8,128)S(1)} %copy-done, f32[512,1024]{1,0:T(8,128)S(1)} %broadcast_select_fusion.top_ref, f32[16,512,512]{2,1,0:T(8,128)} %bitcast.1, f32[8192,1024]{1,0:T(8,128)} %a_ref.3), custom_call_target="tpu_custom_call" | custom-call | tf_op jit(solution)/shard_map/panel_and_update/pallas_call | solution.py:120
Async XLA Ops:
  7.2 213.1 %all-gather.3.cloned.1.call-start = ((), (), s32[]{:S(2)}) async-start(), calls=%async_computation | async-start | bytes 17825792 | tf_op jit(solution)/shard_map/all_gather | solution.py:267
  10.3 64.1 %collective-permute-start.1 = (f32[512,512]{1,0:T(8,128)}, f32[512,512]{1,0:T(8,128)S(1)}, u32[]{:S(2)}, u32[]{:S(2)}) collective-permute-start(f32[512,512]{1,0:T(8,128)} %get-tuple-element.12), channel_id=1, source_target_pairs={{0,1},{1,3},{2,5},{3,7},{4,9},{5,11},{6,13},{7,15},{8,17},{9,19},{... | collective-permute-start | bytes 3145736 | tf_op jit(solution)/shard_map/ppermute | solution.py:261
  12.8 61.6 %collective-permute-start = (f32[512,512]{1,0:T(8,128)}, f32[512,512]{1,0:T(8,128)}, u32[]{:S(2)}, u32[]{:S(2)}) collective-permute-start(f32[512,512]{1,0:T(8,128)} %get-tuple-element.13), channel_id=1, source_target_pairs={{0,0},{1,2},{2,4},{3,6},{4,8},{5,10},{6,12},{7,14},{8,16},{9,18},{... | collective-permute-start | bytes 3145736 | tf_op jit(solution)/shard_map/ppermute | solution.py:261
  24.0 52.9 %copy-start.1 = (f32[512,1024]{1,0:T(8,128)}, f32[512,1024]{1,0:T(8,128)S(1)}, u32[]{:S(2)}) copy-start(f32[512,1024]{1,0:T(8,128)S(1)} %slice.13) | copy-start | bytes 6291460
  76.8 63.5 %collective-permute-start.2 = (f32[512,1024]{1,0:T(8,128)S(1)}, f32[512,1024]{1,0:T(8,128)}, u32[]{:S(2)}, u32[]{:S(2)}) collective-permute-start(f32[512,1024]{1,0:T(8,128)S(1)} %slice.13), channel_id=1, source_target_pairs={{0,16},{1,17},{2,18},{3,19},{4,20},{5,21},{6,22},{7,23},{8,24},{9,... | collective-permute-start | bytes 6291464 | tf_op jit(solution)/shard_map/ppermute | solution.py:270
  140.4 79.9 %copy-start = (f32[512,512]{1,0:T(8,128)S(1)}, f32[512,512]{1,0:T(8,128)}, u32[]{:S(2)}) copy-start(f32[512,512]{1,0:T(8,128)} %inverse_factor.1.w_ref) | copy-start | bytes 3145732
Sparse Core Ops, SparseCore 0:
  77.0 143.3 all-gather.2
